TPU v7x, 32 devices: a 4x4x1 block of a 4x4x8 slice. The times are simulated.
32 devices in a mesh: rep: 1 (over z), row: 4 (over y), col: 4 (over x), core: 2 (over core).
Axes of the slice: x: 4, y: 4, z: 1, core: 2. Of those that a mesh axis runs over, the one named last changes fastest.
The devices are a block of a 4x4x8 slice.
Arguments:
- x: bfloat16 [2, 512, 1280], P(None, ('rep', 'row', 'col', 'core'))
- route_idx: int32 [2, 512, 6], P(None, ('rep', 'row', 'col', 'core'))
- gates: float32 [2, 512, 6], P(None, ('rep', 'row', 'col', 'core'))
- w_gate: bfloat16 [160, 1280, 384], P(('rep', 'row', 'col', 'core'))
- w_up: bfloat16 [160, 1280, 384], P(('rep', 'row', 'col', 'core'))
- w_down: bfloat16 [160, 384, 1280], P(('rep', 'row', 'col', 'core'))
- grad_y: bfloat16 [2, 512, 1280], P(None, ('rep', 'row', 'col', 'core'))
Outputs:
- output 1: bfloat16 [2, 512, 1280], P(None, ('rep', 'row', 'col', 'core'))
- output 2: bfloat16 [2, 512, 1280], P(None, ('rep', 'row', 'col', 'core'))
- output 3: float32 [2, 512, 6], P(None, ('rep', 'row', 'col', 'core'))
- output 4: float32 [160, 1280, 384], P(('rep', 'row', 'col', 'core'))
- output 5: float32 [160, 1280, 384], P(('rep', 'row', 'col', 'core'))
- output 6: float32 [160, 384, 1280], P(('rep', 'row', 'col', 'core'))
All inputs are finite; a program needn't handle non-finite values.
Results may differ from a plain program's by a relative error of at most 0.00984795.
Values are sent between devices in bfloat16 or wider.
A program may use at most 768 MiB of HBM per device.

v0:
```python
import functools

import jax
import jax.numpy as jnp
from jax import lax
from jax.experimental import pallas as pl
from jax.experimental.pallas import tpu as pltpu
from jax.sharding import PartitionSpec as P

GROUP_AXES = ("row", "col", "core")
ALL_AXES = ("rep", "row", "col", "core")
F32 = jnp.float32
BF16 = jnp.bfloat16
LANES = 128
SMALL = 32
EXPERT_VMEM = 49_500_000
COMM_VMEM = 30_000_000


def dot_nn(a, b):
    return lax.dot_general(a, b, (((1,), (0,)), ((), ())), preferred_element_type=F32)


def dot_nt(a, b):
    return lax.dot_general(a, b, (((1,), (1,)), ((), ())), preferred_element_type=F32)


def dot_tn(a, b):
    return lax.dot_general(a, b, (((0,), (0,)), ((), ())), preferred_element_type=F32)


def split3(v):
    h1 = v.astype(BF16)
    r1 = v - h1.astype(F32)
    h2 = r1.astype(BF16)
    h3 = (r1 - h2.astype(F32)).astype(BF16)
    return h1, h2, h3


def col_blocks(width, step):
    return [(s, min(step, width - s)) for s in range(0, width, step)]


def expert_kernel(dims, xd_v, wg_hbm, wu_hbm, wd_hbm, acc_v, gg_hbm, gu_hbm, gd_hbm,
                  pt_v, gr_v, wgu_v, wd_v, og_v, ou_v, od_v, pos_v,
                  xt_v, qt_v, a_v, duv_v, cnt_s, base_s, big_s, sem_w, sem_o):
    tokens, dm, ff, el, top_k, seg = dims
    n_row, n_col, n_core = lax.axis_size("row"), lax.axis_size("col"), lax.axis_size("core")
    me = (lax.axis_index("row") * n_col + lax.axis_index("col")) * n_core + lax.axis_index("core")
    width = 2 * dm + LANES

    def load_w(e):
        pairs = ((wg_hbm, wgu_v.at[e, :, pl.ds(0, ff)]), (wu_hbm, wgu_v.at[e, :, pl.ds(ff, ff)]), (wd_hbm, wd_v.at[e]))
        return [pltpu.make_async_copy(h.at[e], v, sem_w.at[e, i]) for i, (h, v) in enumerate(pairs)]

    def store_g(e, slot):
        return [pltpu.make_async_copy(v.at[slot], h.at[e], sem_o.at[slot, i])
                for i, (h, v) in enumerate(((gg_hbm, og_v), (gu_hbm, ou_v), (gd_hbm, od_v)))]

    for e in range(el):
        for c in load_w(e):
            c.start()

    row_i = lax.broadcasted_iota(jnp.int32, (tokens, tokens), 0)
    col_i = lax.broadcasted_iota(jnp.int32, (tokens, tokens), 1)
    tri = (row_i < col_i).astype(F32).astype(BF16)
    sub = lax.broadcasted_iota(jnp.int32, (8, tokens), 0)
    eids = jnp.where(sub < el, (me * el + sub), -1).astype(F32)

    def chunks(total):
        return jnp.maximum((total + (seg - 1)) // seg, 1)

    n_bigs, n_small = [], []
    for m in range(2):
        meta_t = xd_v[m, :, 2 * dm:].astype(F32).T
        hits = jnp.zeros((8, tokens), F32)
        for j in range(top_k):
            hits = hits + (meta_t[j:j + 1, :] == eids).astype(F32)
        rank = dot_nn(hits.astype(BF16), tri)
        counts = [jnp.sum(hits[e:e + 1, :]).astype(jnp.int32) for e in range(el)]
        n_big = jnp.int32(0)
        for cnt in counts:
            n_big = n_big + (cnt > SMALL).astype(jnp.int32)
        big_at, total = jnp.int32(0), n_big * seg
        for e, cnt in enumerate(counts):
            is_big = cnt > SMALL
            base = jnp.where(is_big, big_at * seg, total)
            cnt_s[m, e] = cnt
            base_s[m, e] = base

            @pl.when(is_big)
            def _(m=m, e=e, big_at=big_at):
                big_s[m, big_at] = jnp.int32(e)

            pos_v[m, e:e + 1, :] = jnp.where(hits[e:e + 1, :] > 0, rank[e:e + 1, :] + base.astype(F32), -1.0)
            big_at = big_at + is_big.astype(jnp.int32)
            total = total + jnp.where(is_big, 0, (cnt + 15) // 16 * 16)
        n_bigs.append(n_big)
        n_small.append(jnp.maximum((total - n_big * seg + (LANES - 1)) // LANES, (n_big == 0).astype(jnp.int32)))
        n_ch = chunks(total)

        def gather(c, carry, m=m):
            off = pl.multiple_of(c * seg, seg)
            rows = (lax.broadcasted_iota(jnp.int32, (seg, tokens), 0) + off).astype(F32)
            pick = rows == pos_v[m, 0:1, :]
            for e in range(1, el):
                pick = pick | (rows == pos_v[m, e:e + 1, :])
            pick_f = pick.astype(F32)
            pt_v[m, :, pl.ds(off, seg)] = pick_f.T.astype(BF16)
            pick_b = pick_f.astype(BF16)
            for s, w in col_blocks(width, 512):
                gr_v[m, pl.ds(off, seg), s:s + w] = dot_nn(pick_b, xd_v[m, :, s:s + w]).astype(BF16)
            return carry

        lax.fori_loop(0, n_ch, gather, 0)

    def tile(e, slot, ra, rb, m_a, n_a, n_b, first):
        rows = ra + rb
        base_a = pl.multiple_of(base_s[m_a, e], 16)
        base_b = pl.multiple_of(base_s[1 - m_a, e], 16)
        it = lax.broadcasted_iota(jnp.int32, (rows, 1), 0)
        valid = ((it < ra) & (it < n_a)) | ((it >= ra) & (it - ra < n_b))

        def read(s, w):
            return jnp.concatenate([gr_v[m_a, pl.ds(base_a, ra), s:s + w],
                                    gr_v[1 - m_a, pl.ds(base_b, rb), s:s + w]], axis=0)

        def write(s, w, val):
            merged = jnp.where(valid, val.astype(F32), read(s, w).astype(F32)).astype(BF16)
            gr_v[m_a, pl.ds(base_a, ra), s:s + w] = merged[:ra]
            gr_v[1 - m_a, pl.ds(base_b, rb), s:s + w] = merged[ra:]

        lane = lax.broadcasted_iota(jnp.int32, (rows, LANES), 1)
        meta = jnp.where(valid, read(2 * dm, LANES).astype(F32), 0.0)
        eid = (me * el + e).astype(F32)
        mine = ((meta == eid) & (lane < top_k)).astype(F32)
        sel = pltpu.roll(mine, 8, 1) + pltpu.roll(mine, 16, 1) + pltpu.roll(mine, 24, 1)
        gate = jnp.where(valid, jnp.sum(meta * sel, axis=1, keepdims=True), 0.0)
        for s, w in col_blocks(dm, 256):
            xt_v[:rows, s:s + w] = jnp.where(valid, read(s, w).astype(F32), 0.0).astype(BF16)
            dy = jnp.where(valid, read(dm + s, w).astype(F32), 0.0)
            qt_v[:rows, s:s + w] = (gate * dy).astype(BF16)
        xt = xt_v[:rows, :]
        uv = dot_nn(xt, wgu_v[e]).astype(BF16).astype(F32)
        u, v = uv[:, :ff], uv[:, ff:]
        r = dot_nt(qt_v[:rows, :], wd_v[e])
        s_g = jax.nn.sigmoid(u)
        a_v[:rows, :] = (u * s_g * v).astype(BF16)
        duv_v[:rows, :ff] = (r * v * s_g * (1.0 + u * (1.0 - s_g))).astype(BF16)
        duv_v[:rows, ff:] = (r * u * s_g).astype(BF16)
        a = a_v[:rows, :]
        duv = duv_v[:rows, :]
        dots = jnp.zeros((rows, 1), F32)
        for s, w in col_blocks(dm, 256):
            o = dot_nn(a, wd_v[e, :, s:s + w]).astype(BF16)
            dy = jnp.where(valid, read(dm + s, w).astype(F32), 0.0)
            dots = dots + jnp.sum(dy * o.astype(F32), axis=1, keepdims=True)
            write(s, w, o)
        for s, w in col_blocks(dm, 256):
            write(dm + s, w, dot_nt(duv, wgu_v[e, s:s + w, :]).astype(BF16))
        d1, d2, d3 = split3(dots)
        g1, g2, g3 = split3(gate)
        new_meta = jnp.zeros((rows, LANES), F32)
        for at, val in ((e, d1), (8 + e, d2), (16 + e, d3), (32, g1), (33, g2), (34, g3)):
            new_meta = jnp.where(lane == at, val.astype(F32), new_meta)
        write(2 * dm, LANES, new_meta)

        def put(ref, idx, val):
            if first is None:
                ref[idx] = val
            else:
                ref[idx] = jnp.where(first, 0.0, ref[idx]) + val

        for s, w in col_blocks(dm, 256):
            g_in = dot_tn(xt_v[:rows, s:s + w], duv)
            put(og_v, (slot, slice(s, s + w)), g_in[:, :ff])
            put(ou_v, (slot, slice(s, s + w)), g_in[:, ff:])
        for s, w in col_blocks(dm, 256):
            put(od_v, (slot, slice(None), slice(s, s + w)), dot_tn(a, qt_v[:rows, s:s + w]))

    def expert(e, carry):
        slot = lax.rem(e, 2)
        for c in load_w(e):
            c.wait()

        @pl.when(e >= 2)
        def _():
            for c in store_g(e - 2, slot):
                c.wait()

        n0, n1 = cnt_s[0, e], cnt_s[1, e]
        big0, big1 = n0 > SMALL, n1 > SMALL

        @pl.when(jnp.logical_not(big0 | big1))
        def _():
            tile(e, slot, SMALL, SMALL, 0, n0, n1, None)

        @pl.when(big0 | big1)
        def _():
            both = big0 & big1

            def one(i, inner):
                m_a = jnp.where(both, i, jnp.where(big0, 0, 1))
                n_a = jnp.where(m_a == 0, n0, n1)
                n_b = jnp.where(both, 0, jnp.where(m_a == 0, n1, n0))
                tile(e, slot, seg, SMALL, m_a, n_a, n_b, i == 0)
                return inner

            lax.fori_loop(0, jnp.where(both, 2, 1), one, 0)

        for c in store_g(e, slot):
            c.start()

        return carry

    lax.fori_loop(0, el, expert, 0)

    for m in range(2):
        lane = lax.broadcasted_iota(jnp.int32, (tokens, LANES), 1)

        def put(s, w, first, add):
            acc_v[m, :, s:s + w] = jnp.where(first, 0.0, acc_v[m, :, s:s + w]) + add

        def back(pt, rows, first):
            for s, w in col_blocks(dm + LANES, 256):
                put(dm + s, w, first, dot_nn(pt, gr_v[m, rows, dm + s:dm + s + w]))

        def one_expert(j, carry):
            rows = pl.ds(pl.multiple_of(j * seg, seg), seg)
            pt = pt_v[m, :, rows]
            meta = xd_v[m, :, 2 * dm:].astype(F32)
            mine = ((meta == (me * el + big_s[m, j]).astype(F32)) & (lane < top_k)).astype(F32)
            sel = pltpu.roll(mine, 8, 1) + pltpu.roll(mine, 16, 1) + pltpu.roll(mine, 24, 1)
            gate = jnp.sum(meta * sel, axis=1, keepdims=True)
            for s, w in col_blocks(dm, 256):
                put(s, w, j == 0, gate * dot_nn(pt, gr_v[m, rows, s:s + w]))
            back(pt, rows, j == 0)
            return carry

        def several(c, carry):
            rows = pl.ds(pl.multiple_of(n_bigs[m] * seg + c * LANES, LANES), LANES)
            first = (c == 0) & (n_bigs[m] == 0)
            pt = pt_v[m, :, rows]
            pt2 = jnp.concatenate([pt, pt], axis=1)
            gp = gr_v[m, rows, 2 * dm:].astype(F32)
            gate = gp[:, 32:33] + gp[:, 33:34] + gp[:, 34:35]
            for s, w in col_blocks(dm, 256):
                h1, h2, h3 = split3(gate * gr_v[m, rows, s:s + w].astype(F32))
                put(s, w, first, dot_nn(pt2, jnp.concatenate([h1, h2], axis=0)) + dot_nn(pt, h3))
            back(pt, rows, first)
            return carry

        lax.fori_loop(0, n_bigs[m], one_expert, 0)
        lax.fori_loop(0, n_small[m], several, 0)
        ids = jnp.where(lane < top_k, xd_v[m, :, 2 * dm:].astype(F32), -1.0)
        raw = acc_v[m, :, 2 * dm:]
        out = jnp.zeros((tokens, LANES), F32)
        for e in range(el):
            val = raw[:, e:e + 1] + raw[:, 8 + e:9 + e] + raw[:, 16 + e:17 + e]
            out = jnp.where(ids == (me * el + e).astype(F32), val, out)
        acc_v[m, :, 2 * dm:] = out

    for e in range(el - 2, el):
        for c in store_g(e, e % 2):
            c.wait()


def expert_stage(xd, w_gate, w_up, w_down, top_k, seg):
    _, tokens, width = xd.shape
    el, dm, ff = w_gate.shape
    any_spec = pl.BlockSpec(memory_space=pltpu.HBM)
    vmem_spec = pl.BlockSpec(memory_space=pltpu.VMEM)
    rows_max = el * seg
    tile_rows = seg + SMALL
    dims = (tokens, dm, ff, el, top_k, seg)
    return pl.pallas_call(
        functools.partial(expert_kernel, dims),
        out_shape=(
            pltpu.VMEM((2, tokens, width), F32),
            pltpu.HBM((el, dm, ff), F32),
            pltpu.HBM((el, dm, ff), F32),
            pltpu.HBM((el, ff, dm), F32),
        ),
        in_specs=[vmem_spec] + [any_spec] * 3,
        out_specs=[vmem_spec] + [any_spec] * 3,
        scratch_shapes=[
            pltpu.VMEM((2, tokens, rows_max), BF16),
            pltpu.VMEM((2, rows_max, width), BF16),
            pltpu.VMEM((el, dm, 2 * ff), BF16),
            pltpu.VMEM((el, ff, dm), BF16),
            pltpu.VMEM((2, dm, ff), F32),
            pltpu.VMEM((2, dm, ff), F32),
            pltpu.VMEM((2, ff, dm), F32),
            pltpu.VMEM((2, 8, tokens), F32),
            pltpu.VMEM((tile_rows, dm), BF16),
            pltpu.VMEM((tile_rows, dm), BF16),
            pltpu.VMEM((tile_rows, ff), BF16),
            pltpu.VMEM((tile_rows, 2 * ff), BF16),
            pltpu.SMEM((2, 8), jnp.int32),
            pltpu.SMEM((2, 8), jnp.int32),
            pltpu.SMEM((2, 8), jnp.int32),
            pltpu.SemaphoreType.DMA((el, 3)),
            pltpu.SemaphoreType.DMA((2, 3)),
        ],
        compiler_params=pltpu.CompilerParams(vmem_limit_bytes=EXPERT_VMEM),
        name="experts",
    )(pltpu.with_memory_space_constraint(xd, pltpu.VMEM), *(pltpu.with_memory_space_constraint(w, pltpu.HBM) for w in (w_gate, w_up, w_down)))


RING = 4
NEAR = (0, -1, 1, 2)
FAR = (2, -1, 1, 0)
GROUPS = (slice(0, 1), slice(1, 3), slice(3, 4))
MESH = pl.DeviceIdType.MESH


class Place:
    def __init__(self):
        self.row, self.col, self.core = (lax.axis_index(a) for a in GROUP_AXES)
        self.n_row, self.n_col = lax.axis_size("row"), lax.axis_size("col")
        self.other = 1 - self.core
        self.partner = {"core": self.other}

    def spot(self, first, d1, d2):
        row = lax.rem(self.row + (d1 * first + d2 * (1 - first)) + self.n_row, self.n_row)
        col = lax.rem(self.col + (d1 * (1 - first) + d2 * first) + self.n_col, self.n_col)
        return row, col

    def peer(self, axis, d):
        row, col = self.spot(self.core, d, 0) if axis == 1 else self.spot(self.core, 0, d)
        return {"row": row, "col": col}

    def barrier(self):
        sem = pltpu.get_barrier_semaphore()
        peers = [self.peer(axis, d) for axis in (1, 2) for d in (1, -1)] + [self.partner]
        for peer in peers:
            pl.semaphore_signal(sem, inc=1, device_id=peer, device_id_type=MESH)
        pl.semaphore_wait(sem, len(peers))


STREAMS = range(2)


def half_lanes(start, size):
    mid = (size // LANES + 1) // 2 * LANES
    return ((start, mid), (start + mid, size - mid))


def stream_lanes(width):
    whole = half_lanes(0, width)
    return [pl.ds(*w) for w in whole], [[pl.ds(*h) for h in half_lanes(*w)] for w in whole]


def token_meta(route, gates):
    top_k, tok_dev = route.shape
    zero = jnp.zeros((8 - top_k, tok_dev), F32)
    parts = [route.astype(F32)] + [p.astype(F32) for p in split3(gates)]
    rows = jnp.concatenate([v for p in parts for v in (p, zero)], axis=0).astype(BF16)
    n = rows.shape[0]
    eye = (lax.broadcasted_iota(jnp.int32, (n, LANES), 0) == lax.broadcasted_iota(jnp.int32, (n, LANES), 1)).astype(F32).astype(BF16)
    return dot_tn(rows, eye).astype(BF16)


def gather_kernel(x_hbm, dy_hbm, route_hbm, gates_hbm, buf, stage, route_v, gates_v, send_sem, recv_sem, load_sem):
    here = Place()
    k, other = here.core, here.other
    dm = x_hbm.shape[2]
    lanes_of, halves = stream_lanes(2 * dm + LANES)
    sent = []

    def move(idx, src, dst, peer):
        return pltpu.make_async_remote_copy(src_ref=src, dst_ref=dst, send_sem=send_sem.at[idx], recv_sem=recv_sem.at[idx],
                                            device_id=peer, device_id_type=MESH)

    def send(idx, src, dst, peer):
        c = move(idx, src, dst, peer)
        c.start()
        sent.append(c)

    def arrive(idx, dst):
        move(idx, dst, dst, here.partner).wait_recv()

    def blk(s, d, g, lanes, side=0):
        ref = buf.at[side, d, g] if s == 0 else buf.at[side, g, d]
        return ref.at[:, :, :, lanes]

    def towards(s, axis, way):
        return here.peer(axis if s == 0 else 3 - axis, 1 - 2 * way)

    class Leg:
        def __init__(self, s, p):
            self.s, self.base, self.axis = s, 37 * s + 6 * p, 1 if p == 0 else 2
            self.at = (lambda j, lanes: blk(s, 0, slice(j, j + 1), lanes)) if p == 0 else (lambda j, lanes: blk(s, j, GROUPS[p - 1], lanes))

        def both_ways(self):
            for way in range(2):
                for n in range(2):
                    lanes = halves[self.s][way if n == 0 else 1 - way]
                    send(self.base + 2 * way + n, self.at(0, lanes), self.at(1 + way, lanes), towards(self.s, self.axis, way))

        def relay(self):
            for way in range(2):
                lanes = halves[self.s][way]
                arrive(self.base + 2 * way, self.at(1 + way, lanes))
                send(self.base + 4 + way, self.at(1 + way, lanes), self.at(3, lanes), towards(self.s, self.axis, way))

        def rest(self):
            for way in range(2):
                arrive(self.base + 2 * way + 1, self.at(1 + way, halves[self.s][1 - way]))

        def far_end(self):
            for way in range(2):
                arrive(self.base + 4 + way, self.at(3, halves[self.s][way]))

    legs = [[Leg(s, p) for p in range(4)] for s in STREAMS]

    def have(s, gi, d):
        lanes = lanes_of[s]
        send(37 * s + 24 + 3 * d + gi, blk(s, d, GROUPS[gi], lanes), blk(s, d, GROUPS[gi], lanes, 1), here.partner)

    def spread(s, gi):
        legs[s][1 + gi].both_ways()
        have(s, gi, 0)

    def second_rest(s, gi):
        legs[s][1 + gi].rest()
        have(s, gi, 1)
        have(s, gi, 2)

    def second_far(s, gi):
        legs[s][1 + gi].far_end()
        have(s, gi, 3)

    mine = buf.at[0, 0, 0, k]
    smalls = [pltpu.make_async_copy(route_hbm, route_v, load_sem.at[4]), pltpu.make_async_copy(gates_hbm, gates_v, load_sem.at[5])]
    loads = [pltpu.make_async_copy(h.at[mb], dst.at[:, pl.ds(lo, dm)], load_sem.at[n])
             for n, (h, mb, dst, lo) in enumerate(((x_hbm, other, stage, 0), (dy_hbm, other, stage, dm), (x_hbm, k, mine, 0), (dy_hbm, k, mine, dm)))]
    for c in smalls + loads:
        c.start()
    for c in smalls:
        c.wait()
    metas = [token_meta(route_v[:, m, :], gates_v[:, m, :]) for m in range(2)]
    zero_core = k == 0
    stage[:, 2 * dm:] = jnp.where(zero_core, metas[1].astype(F32), metas[0].astype(F32)).astype(BF16)
    buf[0, 0, 0, k, :, 2 * dm:] = jnp.where(zero_core, metas[0].astype(F32), metas[1].astype(F32)).astype(BF16)
    here.barrier()
    for c in loads:
        c.wait()
    send(36, stage, buf.at[0, 0, 0, k], here.partner)
    arrive(36, buf.at[0, 0, 0, other])
    for s in STREAMS:
        legs[s][0].both_ways()
    for s in STREAMS:
        spread(s, 0)
    for s in STREAMS:
        legs[s][0].relay()
    for s in STREAMS:
        legs[s][1].relay()
    for s in STREAMS:
        legs[s][0].rest()
        spread(s, 1)
    for s in STREAMS:
        second_rest(s, 0)
    for s in STREAMS:
        legs[s][0].far_end()
        spread(s, 2)
    for s in STREAMS:
        legs[s][2].relay()
    for s in STREAMS:
        second_far(s, 0)
    for s in STREAMS:
        second_rest(s, 1)
    for s in STREAMS:
        legs[s][3].relay()
    for s in STREAMS:
        second_rest(s, 2)
    for s in STREAMS:
        second_far(s, 1)
    for s in STREAMS:
        second_far(s, 2)
    for d in range(RING):
        for gi in range(len(GROUPS)):
            for s in STREAMS:
                arrive(37 * s + 24 + 3 * d + gi, blk(s, d, GROUPS[gi], lanes_of[s], 1))
    for c in sent:
        c.wait_send()


def gather_tokens(x, grad_y, route_idx, gates):
    _, tok_dev, dm = x.shape
    top_k = gates.shape[2]
    width = 2 * dm + LANES
    hbm = pl.BlockSpec(memory_space=pltpu.HBM)
    vmem = pl.BlockSpec(memory_space=pltpu.VMEM)
    sems = pltpu.SemaphoreType.DMA((74,))
    args = (x, grad_y, jnp.transpose(route_idx, (2, 0, 1)), jnp.transpose(gates, (2, 0, 1)))
    return pl.pallas_call(
        gather_kernel,
        out_shape=pltpu.VMEM((2, RING, RING, 2, tok_dev, width), BF16),
        in_specs=[hbm] * 4,
        out_specs=vmem,
        scratch_shapes=[pltpu.VMEM((tok_dev, width), BF16), pltpu.VMEM((top_k, 2, tok_dev), jnp.int32), pltpu.VMEM((top_k, 2, tok_dev), F32),
                        sems, sems, pltpu.SemaphoreType.DMA((6,))],
        compiler_params=pltpu.CompilerParams(collective_id=0, has_side_effects=True, vmem_limit_bytes=COMM_VMEM),
        name="gather_tokens",
    )(*(pltpu.with_memory_space_constraint(v, pltpu.HBM) for v in args))


def reduce_kernel(dm, top_k, part_ref, y_ref, dx_ref, dg_ref, own, pair, full, half, last, pair_send, pair_recv,
                  ring_send, ring_recv, last_sem):
    here = Place()
    k, other = here.core, here.other
    lanes_of, halves = stream_lanes(part_ref.shape[5])
    sent = []

    def slot(s, d, i):
        return (d, i) if s == 0 else (i, d)

    def near_slot(s, d, i):
        return slot(s, NEAR.index(FAR[d]), NEAR.index(FAR[i]))

    def swap(s, d, i):
        lanes = lanes_of[s]
        return pltpu.make_async_remote_copy(src_ref=part_ref.at[(1,) + near_slot(s, d, i)].at[:, :, lanes],
                                            dst_ref=pair.at[slot(s, d, i)].at[:, :, lanes], send_sem=pair_send.at[s, d, i],
                                            recv_sem=pair_recv.at[s, d, i], device_id=here.partner, device_id_type=MESH)

    def move(s, f, kind, src, dst, axis):
        peer = here.peer(axis if s == 0 else 3 - axis, 1 if kind % 2 == 0 else -1)
        return pltpu.make_async_remote_copy(src_ref=src, dst_ref=dst, send_sem=ring_send.at[s, f, kind], recv_sem=ring_recv.at[s, f, kind],
                                            device_id=peer, device_id_type=MESH)

    def go(s, f, kind, src, dst, axis):
        c = move(s, f, kind, src, dst, axis)
        c.start()
        sent.append(c)

    def arrive(s, f, kind, dst):
        move(s, f, kind, dst, dst, 1).wait_recv()

    def own_ref(s, d, g, lanes):
        return own.at[slot(s, d, g)].at[:, :, :, lanes]

    def add_own(s, d, g, lanes, *vals):
        ix = slot(s, d, g) + (slice(None), slice(None), lanes)
        total = own[ix]
        for v in vals:
            total = total + v
        own[ix] = total

    def add_pair(s, d, gi):
        lanes = (slice(None), slice(None), lanes_of[s])
        for i in range(GROUPS[gi].start, GROUPS[gi].stop):
            swap(s, d, i).wait_recv()
            own[slot(s, d, i) + lanes] = part_ref[(0,) + near_slot(s, d, i) + lanes] + pair[slot(s, d, i) + lanes]

    def far(s, f, d, at, g, axis):
        for kind in range(2):
            lanes = halves[s][kind]
            go(s, f, kind, own_ref(s, d, at, lanes), half.at[g, :, :, lanes], axis)

    def near(s, f, spot, g, axis):
        for kind, step in ((0, 1), (1, -1)):
            lanes = halves[s][kind]
            arrive(s, f, kind, half.at[g, :, :, lanes])
            add_own(s, *spot(step), lanes, half[g, :, :, lanes])
        lanes = lanes_of[s]
        for kind, step in ((2, 1), (3, -1)):
            go(s, f, kind, own_ref(s, *spot(step), lanes), full.at[kind - 2, g, :, :, lanes], axis)

    def done(s, f, at, g):
        lanes = lanes_of[s]
        for n in range(2):
            arrive(s, f, 2 + n, full.at[n, g, :, :, lanes])
        add_own(s, 3, at, lanes, full[0, g, :, :, lanes], full[1, g, :, :, lanes])

    def far2(gi):
        for s in STREAMS:
            add_pair(s, 0, gi)
            far(s, gi, 0, GROUPS[gi], GROUPS[gi], 2)

    def near2(gi):
        for s in STREAMS:
            add_pair(s, 2, gi)
            add_pair(s, 1, gi)
        for s in STREAMS:
            near(s, gi, lambda step: (2 if step == 1 else 1, GROUPS[gi]), GROUPS[gi], 2)

    def done2(gi):
        for s in STREAMS:
            add_pair(s, 3, gi)
        for s in STREAMS:
            done(s, gi, GROUPS[gi], GROUPS[gi])

    order = [(0, 0), (0, 1), (0, 2), (2, 0), (1, 0), (0, 3), (2, 1), (2, 2), (1, 1), (1, 2), (3, 0), (2, 3), (1, 3), (3, 1), (3, 2), (3, 3)]
    here.barrier()
    for q in order:
        for s in STREAMS:
            c = swap(s, *q)
            c.start()
            sent.append(c)
    lone = slice(RING, RING + 1)
    far2(0)
    far2(1)
    near2(0)
    far2(2)
    near2(1)
    done2(0)
    for s in STREAMS:
        far(s, 3, 3, slice(0, 1), lone, 1)
    near2(2)
    done2(1)
    for s in STREAMS:
        near(s, 3, lambda step: (3, slice(2, 3) if step == 1 else slice(1, 2)), lone, 1)
    done2(2)
    for s in STREAMS:
        done(s, 3, slice(3, 4), lone)

    give = pltpu.make_async_remote_copy(src_ref=own.at[3, 3, other], dst_ref=last, send_sem=last_sem.at[0], recv_sem=last_sem.at[1],
                                        device_id=here.partner, device_id_type=MESH)
    give.start()
    sent.append(give)

    def emit(mb, val):
        y_ref[mb] = val[:, :dm].astype(BF16)
        dx_ref[mb] = val[:, dm:2 * dm].astype(BF16)
        dg_ref[mb] = val[:, 2 * dm:2 * dm + top_k]

    emit(k, own[3, 3, k])
    give.wait_recv()
    emit(other, last[...])
    for c in sent:
        c.wait_send()


def reduce_tokens(part, dm, top_k):
    _, _, _, cores, tok_dev, width = part.shape
    vmem = pl.BlockSpec(memory_space=pltpu.VMEM)
    block = (cores, tok_dev, width)
    ring_sems = pltpu.SemaphoreType.DMA((2, 4, 4))
    pair_sems = pltpu.SemaphoreType.DMA((2, RING, RING))
    return pl.pallas_call(
        functools.partial(reduce_kernel, dm, top_k),
        out_shape=(
            jax.ShapeDtypeStruct((2, tok_dev, dm), BF16),
            jax.ShapeDtypeStruct((2, tok_dev, dm), BF16),
            jax.ShapeDtypeStruct((2, tok_dev, top_k), F32),
        ),
        in_specs=[vmem],
        out_specs=(vmem, vmem, vmem),
        scratch_shapes=[
            pltpu.VMEM((RING, RING) + block, F32),
            pltpu.VMEM((RING, RING) + block, F32),
            pltpu.VMEM((2, RING + 1) + block, F32),
            pltpu.VMEM((RING + 1,) + block, F32),
            pltpu.VMEM((tok_dev, width), F32),
            pair_sems, pair_sems, ring_sems, ring_sems,
            pltpu.SemaphoreType.DMA((2,)),
        ],
        compiler_params=pltpu.CompilerParams(collective_id=1, has_side_effects=True, vmem_limit_bytes=COMM_VMEM),
        name="reduce_tokens",
    )(pltpu.with_memory_space_constraint(part, pltpu.VMEM))


def solution(mesh):
    group = mesh.shape["row"] * mesh.shape["col"] * mesh.shape["core"]
    tok_spec = P(None, ALL_AXES, None)
    w_spec = P(ALL_AXES, None, None)

    def moe_layer(x, route_idx, gates, w_gate, w_up, w_down, grad_y):
        _, tok_dev, dm = x.shape
        top_k = route_idx.shape[2]
        width = 2 * dm + LANES
        xd = gather_tokens(x, grad_y, route_idx, gates).reshape(2, group * tok_dev, width)
        part, g_gate, g_up, g_down = expert_stage(xd, w_gate, w_up, w_down, top_k, group * (tok_dev // 2))
        y, dx, dg = reduce_tokens(part.reshape(2, RING, RING, 2, tok_dev, width), dm, top_k)
        return y, dx, dg, g_gate, g_up, g_down

    return jax.shard_map(moe_layer, mesh=mesh, in_specs=(tok_spec, tok_spec, tok_spec, w_spec, w_spec, w_spec, tok_spec), out_specs=(tok_spec, tok_spec, tok_spec, w_spec, w_spec, w_spec), check_vma=False)
```

profile of v0, /device:TPU:97, one launch (start us, length us, event | category | flops | bytes accessed | tf_op | source)
XLA Modules:
  0.0 93.3 jit_solution(3140995984421734249)
XLA Ops:
  0.6 28.7 %gather_tokens.1 = bf16[2,4,4,2,16,2688]{5,4,3,2,1,0:T(8,128)(2,1)S(1)} custom-call(bf16[2,16,1280]{2,1,0:T(8,128)(2,1)} %x_hbm.1, bf16[2,16,1280]{2,1,0:T(8,128)(2,1)} %dy_hbm.1, s32[6,2,16]{2,1,0:T(2,128)} %bitcast.6, f32[6,2,16]{2,1,0:T(2,128)} %bitcast.7), custom_call_target="tpu_custom_call" | custom-call | tf_op jit(solution)/shard_map/gather_tokens/pallas_call | solution.py:497
  29.3 19.0 %experts.1 = (f32[2,512,2688]{2,1,0:T(8,128)S(1)}, f32[5,1280,384]{2,1,0:T(8,128)}, f32[5,1280,384]{2,1,0:T(8,128)}, f32[5,384,1280]{2,1,0:T(8,128)}) custom-call(bf16[2,512,2688]{2,1,0:T(8,128)(2,1)S(1)} %bitcast.4, bf16[5,1280,384]{2,1,0:T(8,128)(2,1)} %wg_hbm.1, bf16[5,1280,384]{2,1,0:T(8,128)(2,1)} %wu_hbm.1, bf16[5,384,1280]{2,1,0:T(8,128)(2,1)} %wd_hbm.1), custom_call_target="tpu_custom_call" | custom-call | tf_op jit(solution)/shard_map/experts/pallas_call | solution.py:276
  48.3 43.0 %reduce_tokens.1 = (bf16[2,16,1280]{2,1,0:T(8,128)(2,1)S(1)}, bf16[2,16,1280]{2,1,0:T(8,128)(2,1)S(1)}, f32[2,16,6]{2,1,0:T(8,128)S(1)}) custom-call(f32[2,4,4,2,16,2688]{5,4,3,2,1,0:T(8,128)S(1)} %bitcast.5), custom_call_target="tpu_custom_call" | custom-call | tf_op jit(solution)/shard_map/reduce_tokens/pallas_call | solution.py:642
  91.3 0.7 copy.13
  92.0 0.6 copy.16
  92.6 0.6 copy.17
where the time goes:
time: 93.9 us; the launch traced here: 93.3 us
  Pallas kernels  90.7 us (97%)
  local copies, waits for them, and re-layouts  1.94 us (2%)
    pallas_call x1, Pallas kernels, reduce_tokens(): pl.pallas_call(functools.partial(reduce_kernel, dm, top_k), out_shape=(ja...  43 us
    pallas_call x1, Pallas kernels, gather_tokens(): pl.pallas_call(gather_kernel, out_shape=pltpu.VMEM((2, RING, RING, 2, tok...  28.7 us
    pallas_call x1, Pallas kernels, expert_stage(): pl.pallas_call(functools.partial(expert_kernel, dims), out_shape=(pltpu.V...  19 us
    unnamed x3, local copies, waits for them, and re-layouts  1.94 us

commit v1 on v0

--- a/solution.py
+++ b/solution.py
@@ -57,9 +57,12 @@
         return [pltpu.make_async_copy(v.at[slot], h.at[e], sem_o.at[slot, i])
                 for i, (h, v) in enumerate(((gg_hbm, og_v), (gu_hbm, ou_v), (gd_hbm, od_v)))]
 
-    for e in range(el):
-        for c in load_w(e):
-            c.start()
+    def start_w(lo, hi):
+        for e in range(lo, hi):
+            for c in load_w(e):
+                c.start()
+
+    start_w(0, 1)
 
     row_i = lax.broadcasted_iota(jnp.int32, (tokens, tokens), 0)
     col_i = lax.broadcasted_iota(jnp.int32, (tokens, tokens), 1)
@@ -112,7 +115,9 @@
                 gr_v[m, pl.ds(off, seg), s:s + w] = dot_nn(pick_b, xd_v[m, :, s:s + w]).astype(BF16)
             return carry
 
+        start_w(1 + m, 2 + m)
         lax.fori_loop(0, n_ch, gather, 0)
+    start_w(3, el)
 
     def tile(e, slot, ra, rb, m_a, n_a, n_b, first):
         rows = ra + rb
@@ -506,7 +511,7 @@
     )(*(pltpu.with_memory_space_constraint(v, pltpu.HBM) for v in args))
 
 
-def reduce_kernel(dm, top_k, part_ref, y_ref, dx_ref, dg_ref, own, pair, full, half, last, pair_send, pair_recv,
+def reduce_kernel(part_ref, out_ref, own, pair, full, half, pair_send, pair_recv,
                   ring_send, ring_recv, last_sem):
     here = Place()
     k, other = here.core, here.other
@@ -616,44 +621,54 @@
     for s in STREAMS:
         done(s, 3, slice(3, 4), lone)
 
-    give = pltpu.make_async_remote_copy(src_ref=own.at[3, 3, other], dst_ref=last, send_sem=last_sem.at[0], recv_sem=last_sem.at[1],
+    give = pltpu.make_async_remote_copy(src_ref=own.at[3, 3, other], dst_ref=out_ref.at[k], send_sem=last_sem.at[0], recv_sem=last_sem.at[1],
                                         device_id=here.partner, device_id_type=MESH)
     give.start()
     sent.append(give)
-
-    def emit(mb, val):
-        y_ref[mb] = val[:, :dm].astype(BF16)
-        dx_ref[mb] = val[:, dm:2 * dm].astype(BF16)
-        dg_ref[mb] = val[:, 2 * dm:2 * dm + top_k]
-
-    emit(k, own[3, 3, k])
-    give.wait_recv()
-    emit(other, last[...])
+    out_ref[k] = own[3, 3, k]
+    pltpu.make_async_remote_copy(src_ref=own.at[3, 3, k], dst_ref=out_ref.at[other], send_sem=last_sem.at[0], recv_sem=last_sem.at[1],
+                                 device_id=here.partner, device_id_type=MESH).wait_recv()
     for c in sent:
         c.wait_send()
 
 
-def reduce_tokens(part, dm, top_k):
+def finish_kernel(dm, top_k, in_ref, y_ref, dx_ref, dg_ref):
+    for m in range(2):
+        y_ref[m] = in_ref[m, :, :dm].astype(BF16)
+        dx_ref[m] = in_ref[m, :, dm:2 * dm].astype(BF16)
+        dg_ref[:, m, :] = in_ref[m, :, 2 * dm:].T[:top_k, :]
+
+
+def finish(mine, dm, top_k):
+    _, tok_dev, _ = mine.shape
+    vmem = pl.BlockSpec(memory_space=pltpu.VMEM)
+    out = jax.ShapeDtypeStruct((2, tok_dev, dm), BF16)
+    y, dx, dg = pl.pallas_call(
+        functools.partial(finish_kernel, dm, top_k),
+        out_shape=(out, out, jax.ShapeDtypeStruct((top_k, 2, tok_dev), F32)),
+        in_specs=[vmem],
+        out_specs=(vmem, vmem, vmem),
+        name="finish",
+    )(pltpu.with_memory_space_constraint(mine, pltpu.VMEM))
+    return y, dx, jnp.transpose(dg, (1, 2, 0))
+
+
+def reduce_tokens(part):
     _, _, _, cores, tok_dev, width = part.shape
     vmem = pl.BlockSpec(memory_space=pltpu.VMEM)
     block = (cores, tok_dev, width)
     ring_sems = pltpu.SemaphoreType.DMA((2, 4, 4))
     pair_sems = pltpu.SemaphoreType.DMA((2, RING, RING))
     return pl.pallas_call(
-        functools.partial(reduce_kernel, dm, top_k),
-        out_shape=(
-            jax.ShapeDtypeStruct((2, tok_dev, dm), BF16),
-            jax.ShapeDtypeStruct((2, tok_dev, dm), BF16),
-            jax.ShapeDtypeStruct((2, tok_dev, top_k), F32),
-        ),
+        reduce_kernel,
+        out_shape=pltpu.VMEM((2, tok_dev, width), F32),
         in_specs=[vmem],
-        out_specs=(vmem, vmem, vmem),
+        out_specs=vmem,
         scratch_shapes=[
             pltpu.VMEM((RING, RING) + block, F32),
             pltpu.VMEM((RING, RING) + block, F32),
             pltpu.VMEM((2, RING + 1) + block, F32),
             pltpu.VMEM((RING + 1,) + block, F32),
-            pltpu.VMEM((tok_dev, width), F32),
             pair_sems, pair_sems, ring_sems, ring_sems,
             pltpu.SemaphoreType.DMA((2,)),
         ],
@@ -673,7 +688,7 @@
         width = 2 * dm + LANES
         xd = gather_tokens(x, grad_y, route_idx, gates).reshape(2, group * tok_dev, width)
         part, g_gate, g_up, g_down = expert_stage(xd, w_gate, w_up, w_down, top_k, group * (tok_dev // 2))
-        y, dx, dg = reduce_tokens(part.reshape(2, RING, RING, 2, tok_dev, width), dm, top_k)
+        y, dx, dg = finish(reduce_tokens(part.reshape(2, RING, RING, 2, tok_dev, width)), dm, top_k)
         return y, dx, dg, g_gate, g_up, g_down
 
     return jax.shard_map(moe_layer, mesh=mesh, in_specs=(tok_spec, tok_spec, tok_spec, w_spec, w_spec, w_spec, tok_spec), out_specs=(tok_spec, tok_spec, tok_spec, w_spec, w_spec, w_spec), check_vma=False)

time: 93.9 us -> 92 us (0.980)
  local copies, waits for them, and re-layouts: 1.94 us -> 0 us
    unnamed x3 -> x0, local copies, waits for them, and re-layouts: 1.94 us -> none
    pallas_call x1 -> x2, Pallas kernels: 43 us -> 43.5 us  [the longest x1 42.8 us: reduce_tokens(): pl.pallas_call(reduce_kernel, out_shape=pltpu.VMEM((2, tok_dev, width), F...]
where the time goes in v1:
time: 92 us; the launch traced here: 91.8 us
  Pallas kernels  91.1 us (99%)
    pallas_call x1, Pallas kernels, reduce_tokens(): pl.pallas_call(reduce_kernel, out_shape=pltpu.VMEM((2, tok_dev, width), F...  42.8 us
    pallas_call x1, Pallas kernels, gather_tokens(): pl.pallas_call(gather_kernel, out_shape=pltpu.VMEM((2, RING, RING, 2, tok...  28.7 us
    pallas_call x1, Pallas kernels, expert_stage(): pl.pallas_call(functools.partial(expert_kernel, dims), out_shape=(pltpu.V...  19 us

profile of v1, /device:TPU:97, one launch (start us, length us, event | category | flops | bytes accessed | tf_op | source)
XLA Modules:
  0.0 91.8 jit_solution(15331107871291387016)
XLA Ops:
  0.6 28.7 %gather_tokens.1 = bf16[2,4,4,2,16,2688]{5,4,3,2,1,0:T(8,128)(2,1)S(1)} custom-call(bf16[2,16,1280]{2,1,0:T(8,128)(2,1)} %x_hbm.1, bf16[2,16,1280]{2,1,0:T(8,128)(2,1)} %dy_hbm.1, s32[6,2,16]{2,1,0:T(2,128)} %bitcast.7, f32[6,2,16]{2,1,0:T(2,128)} %bitcast.8), custom_call_target="tpu_custom_call" | custom-call | tf_op jit(solution)/shard_map/gather_tokens/pallas_call | solution.py:502
  29.3 19.0 %experts.1 = (f32[2,512,2688]{2,1,0:T(8,128)S(1)}, f32[5,1280,384]{2,1,0:T(8,128)}, f32[5,1280,384]{2,1,0:T(8,128)}, f32[5,384,1280]{2,1,0:T(8,128)}) custom-call(bf16[2,512,2688]{2,1,0:T(8,128)(2,1)S(1)} %bitcast.5, bf16[5,1280,384]{2,1,0:T(8,128)(2,1)} %wg_hbm.1, bf16[5,1280,384]{2,1,0:T(8,128)(2,1)} %wu_hbm.1, bf16[5,384,1280]{2,1,0:T(8,128)(2,1)} %wd_hbm.1), custom_call_target="tpu_custom_call" | custom-call | tf_op jit(solution)/shard_map/experts/pallas_call | solution.py:281
  48.3 42.8 %reduce_tokens.1.in_ref = f32[2,16,2688]{2,1,0:T(8,128)S(1)} custom-call(f32[2,4,4,2,16,2688]{5,4,3,2,1,0:T(8,128)S(1)} %bitcast.6), custom_call_target="tpu_custom_call" | custom-call | tf_op jit(solution)/shard_map/reduce_tokens/pallas_call | solution.py:662
  91.1 0.7 finish.1
